TPU v7x, 32 devices: a whole 2x2x4 slice. The times are simulated.
32 devices in a mesh: wide: 8 (over z, y), narrow: 2 (over x), grp: 2 (over core).
Axes of the slice: x: 2, y: 2, z: 4, core: 2. Of those that a mesh axis runs over, the one named last changes fastest.
Arguments:
- boundary_block: float32 [8, 2048, 16384], P(None, ('narrow', 'grp'), 'wide'), may hold values from -4 to 4
- schur_blocks: float32 [2, 1536, 1536], P('narrow', ('wide', 'grp')), may hold values from -2 to 2
- interface_rows: int32 [2, 1536], P('narrow'), may hold values from 0 to 8191, as said below
- live_rows: int32 [2], P('narrow'), may hold values from 1 to 1536, 2304 in all
- row_scale: float32 [8, 2048], P('wide', ('narrow', 'grp')), may hold values from 0.4 to 1.2
- excitation: float32 [8, 2048, 128], P('wide', ('narrow', 'grp')), may hold values from -6 to 6
Outputs:
- traces: float32 [8, 2048, 128], P('wide', ('narrow', 'grp'))
- residual: float32 [8, 2048, 128], P('wide', ('narrow', 'grp'))
Inputs may be any that keep to these rules, and one draw needn't show every extreme that they name: `interface_rows`: each substructure's row holds 1536 different positions, 0 to 8191; within each aligned block of 96 slots, at most 32 positions lie in one aligned range of 512 positions, and every substructure reaches 32 in some block.
All inputs are finite; a program needn't handle non-finite values. No bound on the sum of `live_rows` on one device may be relied on, other than what follows from the above.
Results may differ from a plain program's by a relative error of at most 0.00016.
Values sent between devices are 32-bit elements; how exact they have to be, the bound alone decides.
No kernel may reach another device: no remote copies, remote signals or barrier semaphores. Data moves between devices by JAX's collectives and lax.ppermute only.
A program may use at most 128 MiB of HBM per device.

v0:
```python
import jax
import jax.numpy as jnp
from jax import lax
from jax.sharding import PartitionSpec as P

ITERS = 3
RELAX = 0.35


def slot_ranks(owners):
    count = owners.shape[-1]
    same = owners[..., :, None] == owners[..., None, :]
    earlier = jnp.arange(count)[None, :] < jnp.arange(count)[:, None]
    return jnp.sum((same & earlier).astype(jnp.int32), axis=-1)


def on_device(boundary_block, schur_blocks, interface_rows, live_rows, row_scale, excitation):
    piece_rows = excitation.shape[1]
    wide_size = lax.axis_size("wide")
    grp_size = lax.axis_size("grp")
    blocks = wide_size * grp_size
    panel_size = blocks * piece_rows
    tile_block = boundary_block.reshape(-1, boundary_block.shape[2])
    row_weight = row_scale.reshape(piece_rows, 1)
    forcing = excitation[0]
    iface_size = interface_rows.shape[1]
    share_rows = schur_blocks.shape[1]
    sub_count = interface_rows.shape[0]
    row_group = lax.axis_index("wide") * grp_size + lax.axis_index("grp")
    positions = jnp.arange(iface_size, dtype=jnp.int32)
    live_mask = (positions[None, :] < live_rows[:, None]).astype(jnp.float32)
    own_rows = lax.dynamic_slice_in_dim(interface_rows, row_group * share_rows, share_rows, 1)
    slot_cap = (piece_rows + blocks - 1) // blocks
    targets = jnp.arange(blocks, dtype=jnp.int32)
    levels = jnp.arange(slot_cap, dtype=jnp.int32)
    send_owner = own_rows // piece_rows
    send_rank = slot_ranks(send_owner)
    send_pick = (
        (send_owner[:, None, None, :] == targets[None, :, None, None])
        & (send_rank[:, None, None, :] == levels[None, None, :, None])
    ).astype(jnp.float32)
    outgoing = jnp.einsum(
        "kots,ksm->oktm", send_pick, schur_blocks, precision=lax.Precision.HIGHEST
    )
    received = lax.all_to_all(outgoing, ("wide", "grp"), split_axis=0, concat_axis=0, tiled=True)
    block_rows = interface_rows.reshape(sub_count, blocks, share_rows)
    block_live = live_mask.reshape(sub_count, blocks, share_rows)
    block_owner = block_rows // piece_rows
    block_rank = slot_ranks(block_owner)
    take_pick = (
        (block_owner[:, :, None, :] == row_group)
        & (block_rank[:, :, None, :] == levels[None, None, :, None])
    ).astype(jnp.float32) * block_live[:, :, None, :]
    local_index = jnp.arange(piece_rows, dtype=jnp.int32)
    landing = ((block_rows % piece_rows)[..., None] == local_index).astype(jnp.float32)
    placement = jnp.einsum("kjts,kjsi->kjti", take_pick, landing, precision=lax.Precision.HIGHEST)
    traces = RELAX * row_weight * forcing
    residual = forcing
    for sweep in range(ITERS):
        wide_panel = lax.all_gather(traces[None], "wide", axis=0, tiled=True)
        full_panel = lax.all_gather(wide_panel[:, None], "grp", axis=1, tiled=True)
        stacked = wide_panel.reshape(-1, wide_panel.shape[-1])
        boundary = lax.psum_scatter(
            lax.dot_general(
                tile_block,
                stacked,
                (((0,), (0,)), ((), ())),
                precision=lax.Precision.HIGHEST,
                preferred_element_type=jnp.float32,
            ),
            ("narrow", "grp"),
            scatter_dimension=0,
            tiled=True,
        )
        flat_panel = full_panel.reshape(panel_size, -1)
        local_traces = jnp.take(flat_panel, interface_rows, axis=0) * live_mask[:, :, None]
        values = jnp.einsum(
            "jktm,kmr->kjtr", received, local_traces, precision=lax.Precision.HIGHEST
        )
        interface = jnp.einsum("kjti,kjtr->ir", placement, values, precision=lax.Precision.HIGHEST)
        residual = forcing - (boundary + interface)
        traces = traces + RELAX * row_weight * residual
    return (traces[None], residual[None])


def solution(mesh):
    placed = (
        P(None, ("narrow", "grp"), "wide"),
        P("narrow", ("wide", "grp"), None),
        P("narrow", None),
        P("narrow"),
        P("wide", ("narrow", "grp")),
        P("wide", ("narrow", "grp"), None),
    )
    return jax.shard_map(
        on_device,
        mesh=mesh,
        in_specs=placed,
        out_specs=(P("wide", ("narrow", "grp"), None), P("wide", ("narrow", "grp"), None)),
        check_vma=False,
    )
```

profile of v0, /device:TPU:0, one launch (start us, length us, event | category | flops | bytes accessed | tf_op | source)
XLA Modules:
  0.0 362.8 jit_solution(1860652494400219698)
XLA Ops:
  7.2 0.0 all-gather.12.cloned.1.call-start
  7.2 0.7 broadcast_multiply_fusion.1
  8.0 1.8 broadcast_multiply_fusion
  9.8 0.0 all-gather.14.cloned.1.call-start
  9.8 0.8 fusion.56
  10.6 0.2 convert_reduce_fusion.1
  10.8 51.7 %all-gather.12.cloned.1.call-done = f32[8,512,128]{2,1,0:T(8,128)} async-done(((f32[1,512,128]{2,1,0:T(8,128)}), f32[8,512,128]{2,1,0:T(8,128)}) %all-gather.12.cloned.1.call-update) | async-done | bytes 2097168 | tf_op jit(solution)/shard_map/all_gather | solution.py:60
  62.5 0.0 all-gather.14.cloned.1.call-update
  62.6 3.1 convolution_bitcast_fusion
  65.7 4.7 %all-to-all-start = ((f32[16,1,32,1536]{3,2,1,0:T(8,128)}), f32[16,1,32,1536]{3,2,1,0:T(8,128)}, u32[]{:S(2)}, u32[]{:S(2)}) async-start(f32[16,1,32,1536]{3,2,1,0:T(8,128)} %convolution_bitcast_fusion), calls=%async_computation.1 | async-start | bytes 6291456 | tf_op jit(solution)/shard_map/all_to_all | solution.py:45
  70.4 0.0 reduce-scatter.4.cloned.1.call-start
  70.4 23.7 %convolution_bitcast_fusion.3 = f32[2048,128]{0,1:T(8,128)} fusion(f32[8,512,128]{2,1,0:T(8,128)S(1)} %copy-done.2, f32[8,512,2048]{2,1,0:T(8,128)} %param.8), kind=kOutput, calls=%fused_computation.14 | convolution fusion | flops 12884901888 | bytes 36700160 | tf_op jit(solution)/shard_map/dot_general | solution.py:64
  94.2 0.2 all-gather.16.cloned.1.call-start
  94.4 0.1 copy.43
  95.3 0.1 reshape.475
  95.4 0.6 convert_reduce_fusion
  96.0 1.2 fusion.6
  97.3 0.0 all-gather.14.cloned.1.call-done
  97.3 4.8 %gather_fusion = f32[1536,128]{1,0:T(8,128)S(1)} fusion(f32[8192,128]{1,0:T(8,128)} %bitcast.134, s32[2048]{0:T(1024)S(1)} %pad_clamp_fusion), kind=kCustom, calls=%fused_computation.clone | custom fusion | bytes 1579008 | tf_op jit(solution)/shard_map/jit(_take)/gather | solution.py:76
  102.1 27.5 %all-to-all-done = f32[16,1,32,1536]{3,2,1,0:T(8,128)} async-done(((f32[16,1,32,1536]{3,2,1,0:T(8,128)}), f32[16,1,32,1536]{3,2,1,0:T(8,128)}, u32[]{:S(2)}, u32[]{:S(2)}) %all-to-all-start) | async-done | bytes 3145760 | tf_op jit(solution)/shard_map/all_to_all | solution.py:45
  129.6 4.6 %fusion.4 = f32[16,32,128]{2,1,0:T(8,128)S(1)} fusion(f32[16,1,32,1536]{3,2,1,0:T(8,128)} %all-to-all-done, f32[1536,128]{1,0:T(8,128)S(1)} %gather_fusion, f32[1536]{0:T(1024)S(1)} %fusion.54, pred[1536]{0:T(1024)(128)(4,1)S(1)} %and_reduce_fusion), kind=kOutput, calls=%fused_computation.8 | convolution fusion | flops 1208352768 | bytes 4201984 | tf_op jit(solution)/shard_map/jktm,kmr->kjtr/dot_general | solution.py:77
  134.2 0.0 reduce-scatter.4.cloned.1.call-done
  134.2 2.5 fusion.15
  136.7 0.0 all-gather.18.cloned.1.call-start
  136.8 59.9 %all-gather.16.cloned.1.call-done = f32[4096,128]{0,1:T(8,128)} async-done(((f32[512,128]{0,1:T(8,128)}), f32[4096,128]{0,1:T(8,128)}) %all-gather.16.cloned.1.call-update) | async-done | bytes 2097168 | tf_op jit(solution)/shard_map/all_gather | solution.py:60
  196.6 4.6 %copy.64 = f32[16,8,8,512]{3,2,1,0:T(8,128)} copy(f32[16,8,8,512]{3,1,2,0:T(8,128)} %bitcast.135) | data formatting | bytes 4194304
  201.2 0.3 reduce-scatter.6.cloned.1.call-start
  201.5 23.8 %convolution_bitcast_fusion.2 = f32[2048,128]{0,1:T(8,128)} fusion(f32[8,512,2048]{2,1,0:T(8,128)} %param.8, f32[16,8,8,512]{3,2,1,0:T(8,128)} %bitcast.136), kind=kOutput, calls=%fused_computation.13 | convolution fusion | flops 12884901888 | bytes 36700160 | tf_op jit(solution)/shard_map/dot_general | solution.py:64
  225.3 0.0 all-gather.20.cloned.1.call-start
  225.3 0.0 all-gather.18.cloned.1.call-done
  225.4 5.4 %copy.48 = f32[8,1024,128]{2,1,0:T(8,128)} copy(f32[8,1024,128]{1,0,2:T(8,128)} %all-gather.18.cloned.1.call-done) | data formatting | bytes 8388608 | tf_op jit(solution)/shard_map/all_gather | solution.py:61
  230.7 4.9 %gather_fusion.1 = f32[1536,128]{1,0:T(8,128)S(1)} fusion(f32[8192,128]{1,0:T(8,128)} %bitcast.133, s32[2048]{0:T(1024)S(1)} %pad_clamp_fusion), kind=kCustom, calls=%fused_computation.1.clone | custom fusion | bytes 1579008 | tf_op jit(solution)/shard_map/jit(_take)/gather | solution.py:76
  235.7 4.7 %fusion.2 = f32[16,32,128]{2,1,0:T(8,128)S(1)} fusion(f32[16,1,32,1536]{3,2,1,0:T(8,128)} %all-to-all-done, f32[1536,128]{1,0:T(8,128)S(1)} %gather_fusion.1, f32[1536]{0:T(1024)S(1)} %fusion.54, pred[1536]{0:T(1024)(128)(4,1)S(1)} %and_reduce_fusion), kind=kOutput, calls=%fused_computation.6 | convolution fusion | flops 1208352768 | bytes 4201984 | tf_op jit(solution)/shard_map/jktm,kmr->kjtr/dot_general | solution.py:77
  240.4 8.4 %reduce-scatter.6.cloned.1.call-done = f32[512,128]{0,1:T(8,128)} async-done(((f32[2048,128]{0,1:T(8,128)}), f32[512,128]{0,1:T(8,128)}) %reduce-scatter.6.cloned.1.call-update) | async-done | bytes 262160 | tf_op jit(solution)/shard_map/reduce_scatter | solution.py:63
  248.7 2.5 fusion.19
  251.2 0.0 all-gather.22.cloned.1.call-start
  251.3 49.3 %all-gather.20.cloned.1.call-done = f32[4096,128]{0,1:T(8,128)} async-done(((f32[512,128]{0,1:T(8,128)}), f32[4096,128]{0,1:T(8,128)}) %all-gather.20.cloned.1.call-update) | async-done | bytes 2097168 | tf_op jit(solution)/shard_map/all_gather | solution.py:60
  300.6 4.6 %copy.65 = f32[16,8,8,512]{3,2,1,0:T(8,128)} copy(f32[16,8,8,512]{3,1,2,0:T(8,128)} %bitcast.137) | data formatting | bytes 4194304
  305.2 0.3 reduce-scatter.8.cloned.1.call-start
  305.5 23.8 %convolution_bitcast_fusion.1 = f32[2048,128]{0,1:T(8,128)} fusion(f32[8,512,2048]{2,1,0:T(8,128)} %param.8, f32[16,8,8,512]{3,2,1,0:T(8,128)} %bitcast.138), kind=kOutput, calls=%fused_computation.12 | convolution fusion | flops 12884901888 | bytes 36700160 | tf_op jit(solution)/shard_map/dot_general | solution.py:64
  329.3 0.0 all-gather.22.cloned.1.call-done
  329.3 5.4 %copy.51 = f32[8,1024,128]{2,1,0:T(8,128)} copy(f32[8,1024,128]{1,0,2:T(8,128)} %all-gather.22.cloned.1.call-done) | data formatting | bytes 8388608 | tf_op jit(solution)/shard_map/all_gather | solution.py:61
  334.7 5.0 %gather_fusion.2 = f32[1536,128]{1,0:T(8,128)S(1)} fusion(f32[8192,128]{1,0:T(8,128)} %bitcast.132, s32[2048]{0:T(1024)S(1)} %pad_clamp_fusion), kind=kCustom, calls=%fused_computation.2.clone | custom fusion | bytes 1579008 | tf_op jit(solution)/shard_map/jit(_take)/gather | solution.py:76
  339.8 4.7 %fusion = f32[16,32,128]{2,1,0:T(8,128)S(1)} fusion(f32[16,1,32,1536]{3,2,1,0:T(8,128)} %all-to-all-done, f32[1536,128]{1,0:T(8,128)S(1)} %gather_fusion.2, f32[1536]{0:T(1024)S(1)} %fusion.54, pred[1536]{0:T(1024)(128)(4,1)S(1)} %and_reduce_fusion), kind=kOutput, calls=%fused_computation.4 | convolution fusion | flops 1208352768 | bytes 4201984 | tf_op jit(solution)/shard_map/jktm,kmr->kjtr/dot_general | solution.py:77
  344.4 8.4 %reduce-scatter.8.cloned.1.call-done = f32[512,128]{0,1:T(8,128)} async-done(((f32[2048,128]{0,1:T(8,128)}), f32[512,128]{0,1:T(8,128)}) %reduce-scatter.8.cloned.1.call-update) | async-done | bytes 262160 | tf_op jit(solution)/shard_map/reduce_scatter | solution.py:63
  352.8 1.7 fusion.21
  354.6 0.8 copy.53
  355.4 0.8 copy.54
  (33 shorter events, 0.4 us)
Async XLA Ops:
  7.2 55.4 %copy-start = (f32[1,96,1536]{2,1,0:T(8,128)S(1)}, f32[1,96,1536]{2,1,0:T(8,128)}, u32[]{:S(2)}) copy-start(f32[1,96,1536]{2,1,0:T(8,128)} %param.9) | copy-start | bytes 1769476
  7.2 55.3 %all-gather.12.cloned.1.call-start = ((), (), s32[]{:S(2)}) async-start(), calls=%async_computation.4 | async-start | bytes 2359296 | tf_op jit(solution)/shard_map/all_gather | solution.py:60
  9.8 87.5 %all-gather.14.cloned.1.call-start = ((), (), s32[]{:S(2)}) async-start(), calls=%async_computation.8 | async-start | bytes 6291456 | tf_op jit(solution)/shard_map/all_gather | solution.py:61
  65.7 4.8 %copy-start.2 = (f32[8,512,128]{2,1,0:T(8,128)S(1)}, f32[8,512,128]{2,1,0:T(8,128)}, u32[]{:S(2)}) copy-start(f32[8,512,128]{2,1,0:T(8,128)} %all-gather.12.cloned.1.call-done) | copy-start | bytes 6291460
  65.7 63.9 %all-to-all-start = ((f32[16,1,32,1536]{3,2,1,0:T(8,128)}), f32[16,1,32,1536]{3,2,1,0:T(8,128)}, u32[]{:S(2)}, u32[]{:S(2)}) async-start(f32[16,1,32,1536]{3,2,1,0:T(8,128)} %convolution_bitcast_fusion), calls=%async_computation.1 | async-start | bytes 6291456 | tf_op jit(solution)/shard_map/all_to_all | solution.py:45
  70.4 24.1 %copy-start.5 = (f32[1,512,128]{2,1,0:T(8,128)S(1)}, f32[1,512,128]{2,1,0:T(8,128)}, u32[]{:S(2)}) copy-start(f32[1,512,128]{2,1,0:T(8,128)} %param.13) | copy-start | bytes 786436
  70.4 24.8 %copy-start.6 = (s32[1,1536]{1,0:T(1,128)S(1)}, s32[1,1536]{1,0:T(1,128)}, u32[]{:S(2)}) copy-start(s32[1,1536]{1,0:T(1,128)} %param.10) | copy-start | bytes 18436
  70.4 63.8 %reduce-scatter.4.cloned.1.call-start = ((), (), s32[]{:S(2)}) async-start(), calls=%async_computation.5 | async-start | bytes 1310720 | tf_op jit(solution)/shard_map/reduce_scatter | solution.py:63
  94.2 102.5 %all-gather.16.cloned.1.call-start = ((), (), s32[]{:S(2)}) async-start(), calls=%async_computation.9 | async-start | bytes 2359296 | tf_op jit(solution)/shard_map/all_gather | solution.py:60
  136.7 88.6 %all-gather.18.cloned.1.call-start = ((), (), s32[]{:S(2)}) async-start(), calls=%async_computation.10 | async-start | bytes 6291456 | tf_op jit(solution)/shard_map/all_gather | solution.py:61
  201.2 47.5 %reduce-scatter.6.cloned.1.call-start = ((), (), s32[]{:S(2)}) async-start(), calls=%async_computation.6 | async-start | bytes 1310720 | tf_op jit(solution)/shard_map/reduce_scatter | solution.py:63
  225.3 75.3 %all-gather.20.cloned.1.call-start = ((), (), s32[]{:S(2)}) async-start(), calls=%async_computation.11 | async-start | bytes 2359296 | tf_op jit(solution)/shard_map/all_gather | solution.py:60
  235.7 13.1 %copy-start.4 = (f32[512,128]{0,1:T(8,128)S(1)}, f32[512,128]{0,1:T(8,128)}, u32[]{:S(2)}) copy-start(f32[512,128]{0,1:T(8,128)} %fusion.15) | copy-start | bytes 786436
  251.2 78.1 %all-gather.22.cloned.1.call-start = ((), (), s32[]{:S(2)}) async-start(), calls=%async_computation.12 | async-start | bytes 6291456 | tf_op jit(solution)/shard_map/all_gather | solution.py:61
  305.2 47.6 %reduce-scatter.8.cloned.1.call-start = ((), (), s32[]{:S(2)}) async-start(), calls=%async_computation.7 | async-start | bytes 1310720 | tf_op jit(solution)/shard_map/reduce_scatter | solution.py:63
  334.7 21.5 %copy-start.1 = (f32[1,96,1536]{2,1,0:T(8,128)S(1)}, f32[1,96,1536]{2,1,0:T(8,128)}, u32[]{:S(2)}) copy-start(f32[1,96,1536]{2,1,0:T(8,128)} %param.9) | copy-start | bytes 1769476
  339.7 14.8 %copy-start.3 = (f32[512,128]{0,1:T(8,128)S(1)}, f32[512,128]{0,1:T(8,128)}, u32[]{:S(2)}) copy-start(f32[512,128]{0,1:T(8,128)} %fusion.19) | copy-start | bytes 786436
Sparse Core Ops, SparseCore 0:
  10.7 51.7 all-gather.11
  64.1 12.1 all-gather.13
  94.3 25.9 reduce-scatter.3
  136.8 59.7 all-gather.15
  201.3 12.1 all-gather.17
  225.4 23.2 reduce-scatter.5
  251.5 49.0 all-gather.19
  305.3 12.1 all-gather.21
  329.4 23.2 reduce-scatter.7
where the time goes:
time: 363 us
  waiting for transfers between devices  205 us (56%)
  matrix products  96.2 us (27%)
  local copies, waits for them, and re-layouts  36.5 us (10%)
  between operations  14.8 us (4%)
  starting transfers between devices  5.72 us (2%)
  other arithmetic  4.22 us (1%)
    all_gather x3, waiting for transfers between devices, on_device(): wide_panel = lax.all_gather(traces[None], 'wide', axis=0, tiled=True)  161 us
    dot_general x3, matrix products, on_device(): lax.dot_general(tile_block, stacked, (((0,), (0,)), ((), ())), precision=...  71.2 us
    all_to_all x1, waiting for transfers between devices, on_device(): lax.all_to_all(outgoing, ('wide', 'grp'), split_axis=0, concat_axis=0, ti...  27.5 us
    reduce_scatter x3, waiting for transfers between devices, on_device(): lax.psum_scatter(lax.dot_general(tile_block, stacked, (((0,), (0,)), ((),...  16.8 us
    gather x3, local copies, waits for them, and re-layouts, on_device(): jnp.take(flat_panel, interface_rows, axis=0) * live_mask[:, :, None]  14.7 us
    dot_general x3, matrix products, on_device(): jnp.einsum('jktm,kmr->kjtr', received, local_traces, precision=lax.Precis...  13.9 us
    unnamed x19, local copies, waits for them, and re-layouts  11 us
    all_gather x2, local copies, waits for them, and re-layouts, on_device(): full_panel = lax.all_gather(wide_panel[:, None], 'grp', axis=1, tiled=True)  10.8 us
  transfers between devices with their start and end apart: 10, of which 6 were waited for; matrix products, arithmetic and copies ran while one was open for 32% of the time, Pallas kernels for 0%

commit v1 on v0

--- a/solution.py
+++ b/solution.py
@@ -57,7 +57,14 @@
     traces = RELAX * row_weight * forcing
     residual = forcing
     for sweep in range(ITERS):
-        wide_panel = lax.all_gather(traces[None], "wide", axis=0, tiled=True)
+        ring = [traces[None]]
+        for hop in range(7):
+            ring.append(lax.ppermute(ring[-1], "wide", [(dev, (dev + 1) % 8) for dev in range(8)]))
+        wide_panel = jnp.roll(
+            jnp.concatenate(ring[::-1], axis=0),
+            (lax.axis_index("wide") + 1) * ring[0].shape[0],
+            axis=0,
+        )
         full_panel = lax.all_gather(wide_panel[:, None], "grp", axis=1, tiled=True)
         stacked = wide_panel.reshape(-1, wide_panel.shape[-1])
         boundary = lax.psum_scatter(

time: 363 us -> 399 us (1.099)
  waiting for transfers between devices: 205 us -> 224 us
  starting transfers between devices: 5.72 us -> 16.2 us
  other arithmetic: 4.22 us -> 11.2 us
  matrix products: 96.2 us -> 90.5 us
    ppermute x0 -> x21, waiting for transfers between devices: none -> 194 us  [on_device(): lax.ppermute(ring[-1], 'wide', [(dev, (dev + 1) % 8) for dev in range(8)])]
    all_gather x3 -> x0, waiting for transfers between devices: 161 us -> none  [on_device(): wide_panel = lax.all_gather(traces[None], 'wide', axis=0, tiled=True)]
    ppermute x0 -> x21, starting transfers between devices: none -> 9.44 us  [on_device(): lax.ppermute(ring[-1], 'wide', [(dev, (dev + 1) % 8) for dev in range(8)])]
    all_to_all x1, waiting for transfers between devices: 27.5 us -> 19.3 us  [on_device(): lax.all_to_all(outgoing, ('wide', 'grp'), split_axis=0, concat_axis=0, ti...]
    reduce_scatter x3, waiting for transfers between devices: 16.8 us -> 10 us  [on_device(): lax.psum_scatter(lax.dot_general(tile_block, stacked, (((0,), (0,)), ((),...]
    all_gather x2 -> x3, local copies, waits for them, and re-layouts: 10.8 us -> 16.9 us  [on_device(): full_panel = lax.all_gather(wide_panel[:, None], 'grp', axis=1, tiled=True)]
    concatenate x0 -> x4, other arithmetic: none -> 5.67 us  [the longest x3 5.65 us: on_device(): jnp.roll(jnp.concatenate(ring[::-1], axis=0), (lax.axis_index('wide') + 1...]
    dot_general x3, matrix products: 6.67 us -> 2.4 us  [on_device(): jnp.einsum('kjti,kjtr->ir', placement, values, precision=lax.Precision.HI...]
  transfers between devices with their start and end apart: 10 -> 28, of which waited for: 6 -> 23; matrix products, arithmetic and copies ran while one was open for 32% -> 32% of each run, Pallas kernels for 0% -> 0%
where the time goes in v1:
time: 399 us; the launch traced here: 398 us
  waiting for transfers between devices  224 us (56%)
  matrix products  90.5 us (23%)
  local copies, waits for them, and re-layouts  39.2 us (10%)
  between operations  16.6 us (4%)
  starting transfers between devices  16.2 us (4%)
  other arithmetic  11.2 us (3%)
    ppermute x21, waiting for transfers between devices, on_device(): lax.ppermute(ring[-1], 'wide', [(dev, (dev + 1) % 8) for dev in range(8)])  194 us
    dot_general x3, matrix products, on_device(): lax.dot_general(tile_block, stacked, (((0,), (0,)), ((), ())), precision=...  69.6 us
    all_to_all x1, waiting for transfers between devices, on_device(): lax.all_to_all(outgoing, ('wide', 'grp'), split_axis=0, concat_axis=0, ti...  19.3 us
    all_gather x3, local copies, waits for them, and re-layouts, on_device(): full_panel = lax.all_gather(wide_panel[:, None], 'grp', axis=1, tiled=True)  16.9 us
    gather x3, local copies, waits for them, and re-layouts, on_device(): jnp.take(flat_panel, interface_rows, axis=0) * live_mask[:, :, None]  14.4 us
    dot_general x3, matrix products, on_device(): jnp.einsum('jktm,kmr->kjtr', received, local_traces, precision=lax.Precis...  14.2 us
    reduce_scatter x3, waiting for transfers between devices, on_device(): lax.psum_scatter(lax.dot_general(tile_block, stacked, (((0,), (0,)), ((),...  10 us
    ppermute x21, starting transfers between devices, on_device(): lax.ppermute(ring[-1], 'wide', [(dev, (dev + 1) % 8) for dev in range(8)])  9.44 us
  transfers between devices with their start and end apart: 28, of which 23 were waited for; matrix products, arithmetic and copies ran while one was open for 32% of the time, Pallas kernels for 0%

profile of v1, /device:TPU:0, one launch (start us, length us, event | category | flops | bytes accessed | tf_op | source)
XLA Modules:
  0.0 397.7 jit_solution(394294983996259930)
XLA Ops:
  8.0 1.1 copy.36
  9.9 3.0 collective-permute-start
  12.9 9.3 %collective-permute-done = f32[1,512,128]{1,2,0:T(8,128)S(1)} collective-permute-done((f32[1,512,128]{1,2,0:T(8,128)S(1)}, f32[1,512,128]{1,2,0:T(8,128)S(1)}, u32[]{:S(2)}, u32[]{:S(2)}) %collective-permute-start) | collective-permute-done | bytes 262176 | tf_op jit(solution)/shard_map/ppermute | solution.py:62
  22.3 10.2 %collective-permute-done.1 = f32[1,512,128]{1,2,0:T(8,128)S(1)} collective-permute-done((f32[1,512,128]{1,2,0:T(8,128)S(1)}, f32[1,512,128]{1,2,0:T(8,128)S(1)}, u32[]{:S(2)}, u32[]{:S(2)}) %collective-permute-start.1) | collective-permute-done | bytes 262176 | tf_op jit(solution)/shard_map/ppermute | solution.py:62
  32.4 9.3 %collective-permute-done.2 = f32[1,512,128]{1,2,0:T(8,128)S(1)} collective-permute-done((f32[1,512,128]{1,2,0:T(8,128)S(1)}, f32[1,512,128]{1,2,0:T(8,128)S(1)}, u32[]{:S(2)}, u32[]{:S(2)}) %collective-permute-start.2) | collective-permute-done | bytes 262176 | tf_op jit(solution)/shard_map/ppermute | solution.py:62
  41.7 9.1 %collective-permute-done.3 = f32[1,512,128]{1,2,0:T(8,128)S(1)} collective-permute-done((f32[1,512,128]{1,2,0:T(8,128)S(1)}, f32[1,512,128]{1,2,0:T(8,128)S(1)}, u32[]{:S(2)}, u32[]{:S(2)}) %collective-permute-start.3) | collective-permute-done | bytes 262176 | tf_op jit(solution)/shard_map/ppermute | solution.py:62
  51.6 8.3 %collective-permute-done.4 = f32[1,512,128]{1,2,0:T(8,128)S(1)} collective-permute-done((f32[1,512,128]{1,2,0:T(8,128)S(1)}, f32[1,512,128]{1,2,0:T(8,128)S(1)}, u32[]{:S(2)}, u32[]{:S(2)}) %collective-permute-start.4) | collective-permute-done | bytes 262176 | tf_op jit(solution)/shard_map/ppermute | solution.py:62
  60.1 9.5 %collective-permute-done.5 = f32[1,512,128]{1,2,0:T(8,128)S(1)} collective-permute-done((f32[1,512,128]{1,2,0:T(8,128)S(1)}, f32[1,512,128]{1,2,0:T(8,128)S(1)}, u32[]{:S(2)}, u32[]{:S(2)}) %collective-permute-start.5) | collective-permute-done | bytes 262176 | tf_op jit(solution)/shard_map/ppermute | solution.py:62
  69.6 3.1 convolution_bitcast_fusion
  72.7 6.1 %all-to-all-start = ((f32[16,1,32,1536]{3,2,1,0:T(8,128)}), f32[16,1,32,1536]{3,2,1,0:T(8,128)}, u32[]{:S(2)}, u32[]{:S(2)}) async-start(f32[16,1,32,1536]{3,2,1,0:T(8,128)} %convolution_bitcast_fusion), calls=%async_computation.1 | async-start | bytes 6291456 | tf_op jit(solution)/shard_map/all_to_all | solution.py:45
  79.1 1.9 fusion.9
  81.1 1.5 copy-done.2
  82.6 22.5 %convolution_bitcast_fusion.3 = f32[2048,128]{0,1:T(8,128)} fusion(f32[8,512,128]{1,2,0:T(8,128)S(1)} %copy-done.2, f32[8,512,2048]{2,1,0:T(8,128)} %param.10), kind=kOutput, calls=%fused_computation.20 | convolution fusion | flops 12884901888 | bytes 36700160 | tf_op jit(solution)/shard_map/dot_general | solution.py:71
  106.9 1.2 fusion.6
  108.2 5.8 %copy.39 = f32[8,1024,128]{2,1,0:T(8,128)} copy(f32[8,1024,128]{1,2,0:T(8,128)} %all-gather.7.cloned.1.call-done) | data formatting | bytes 8388608 | tf_op jit(solution)/shard_map/all_gather | solution.py:68
  114.0 4.9 %gather_fusion = f32[1536,128]{1,0:T(8,128)S(1)} fusion(f32[8192,128]{1,0:T(8,128)} %bitcast.116, s32[2048]{0:T(1024)S(1)} %pad_clamp_fusion), kind=kCustom, calls=%fused_computation.clone | custom fusion | bytes 1579008 | tf_op jit(solution)/shard_map/jit(_take)/gather | solution.py:83
  118.8 19.3 %all-to-all-done = f32[16,1,32,1536]{3,2,1,0:T(8,128)} async-done(((f32[16,1,32,1536]{3,2,1,0:T(8,128)}), f32[16,1,32,1536]{3,2,1,0:T(8,128)}, u32[]{:S(2)}, u32[]{:S(2)}) %all-to-all-start) | async-done | bytes 3145760 | tf_op jit(solution)/shard_map/all_to_all | solution.py:45
  138.1 4.6 %fusion.4 = f32[16,32,128]{2,1,0:T(8,128)S(1)} fusion(f32[16,1,32,1536]{3,2,1,0:T(8,128)} %all-to-all-done, f32[1536,128]{1,0:T(8,128)S(1)} %gather_fusion, f32[1536]{0:T(1024)S(1)} %fusion.47, pred[1536]{0:T(1024)(128)(4,1)S(1)} %and_reduce_fusion), kind=kOutput, calls=%fused_computation.14 | convolution fusion | flops 1208352768 | bytes 4201984 | tf_op jit(solution)/shard_map/jktm,kmr->kjtr/dot_general | solution.py:84
  144.6 4.8 %collective-permute-start.7 = (f32[1,512,128]{1,2,0:T(8,128)S(1)}, f32[1,512,128]{1,2,0:T(8,128)S(1)}, u32[]{:S(2)}, u32[]{:S(2)}) collective-permute-start(f32[1,512,128]{1,2,0:T(8,128)S(1)} %fusion.43), channel_id=1, source_target_pairs={{0,4},{4,8},{8,12},{12,16},{16,20},{20,24},{24,28},{28,0},{1,5},{5... | collective-permute-start | bytes 786440 | tf_op jit(solution)/shard_map/ppermute | solution.py:62
  149.5 16.1 %collective-permute-done.7 = f32[1,512,128]{1,2,0:T(8,128)S(1)} collective-permute-done((f32[1,512,128]{1,2,0:T(8,128)S(1)}, f32[1,512,128]{1,2,0:T(8,128)S(1)}, u32[]{:S(2)}, u32[]{:S(2)}) %collective-permute-start.7) | collective-permute-done | bytes 262176 | tf_op jit(solution)/shard_map/ppermute | solution.py:62
  165.6 10.7 %collective-permute-done.8 = f32[1,512,128]{1,2,0:T(8,128)S(1)} collective-permute-done((f32[1,512,128]{1,2,0:T(8,128)S(1)}, f32[1,512,128]{1,2,0:T(8,128)S(1)}, u32[]{:S(2)}, u32[]{:S(2)}) %collective-permute-start.8) | collective-permute-done | bytes 262176 | tf_op jit(solution)/shard_map/ppermute | solution.py:62
  176.3 9.9 %collective-permute-done.9 = f32[1,512,128]{1,2,0:T(8,128)S(1)} collective-permute-done((f32[1,512,128]{1,2,0:T(8,128)S(1)}, f32[1,512,128]{1,2,0:T(8,128)S(1)}, u32[]{:S(2)}, u32[]{:S(2)}) %collective-permute-start.9) | collective-permute-done | bytes 262176 | tf_op jit(solution)/shard_map/ppermute | solution.py:62
  186.2 9.1 %collective-permute-done.10 = f32[1,512,128]{1,2,0:T(8,128)S(1)} collective-permute-done((f32[1,512,128]{1,2,0:T(8,128)S(1)}, f32[1,512,128]{1,2,0:T(8,128)S(1)}, u32[]{:S(2)}, u32[]{:S(2)}) %collective-permute-start.10) | collective-permute-done | bytes 262176 | tf_op jit(solution)/shard_map/ppermute | solution.py:62
  195.3 9.1 %collective-permute-done.11 = f32[1,512,128]{1,2,0:T(8,128)S(1)} collective-permute-done((f32[1,512,128]{1,2,0:T(8,128)S(1)}, f32[1,512,128]{1,2,0:T(8,128)S(1)}, u32[]{:S(2)}, u32[]{:S(2)}) %collective-permute-start.11) | collective-permute-done | bytes 262176 | tf_op jit(solution)/shard_map/ppermute | solution.py:62
  204.3 9.1 %collective-permute-done.12 = f32[1,512,128]{1,2,0:T(8,128)S(1)} collective-permute-done((f32[1,512,128]{1,2,0:T(8,128)S(1)}, f32[1,512,128]{1,2,0:T(8,128)S(1)}, u32[]{:S(2)}, u32[]{:S(2)}) %collective-permute-start.12) | collective-permute-done | bytes 262176 | tf_op jit(solution)/shard_map/ppermute | solution.py:62
  213.4 9.1 %collective-permute-done.13 = f32[1,512,128]{1,2,0:T(8,128)S(1)} collective-permute-done((f32[1,512,128]{1,2,0:T(8,128)S(1)}, f32[1,512,128]{1,2,0:T(8,128)S(1)}, u32[]{:S(2)}, u32[]{:S(2)}) %collective-permute-start.13) | collective-permute-done | bytes 262176 | tf_op jit(solution)/shard_map/ppermute | solution.py:62
  222.7 1.9 fusion.8
  224.7 1.5 copy-done.3
  226.2 23.4 %convolution_bitcast_fusion.2 = f32[2048,128]{0,1:T(8,128)} fusion(f32[8,512,128]{1,2,0:T(8,128)S(1)} %copy-done.3, f32[8,512,2048]{2,1,0:T(8,128)} %param.10), kind=kOutput, calls=%fused_computation.19 | convolution fusion | flops 12884901888 | bytes 36700160 | tf_op jit(solution)/shard_map/dot_general | solution.py:71
  249.9 5.5 %copy.41 = f32[8,1024,128]{2,1,0:T(8,128)} copy(f32[8,1024,128]{1,2,0:T(8,128)} %all-gather.9.cloned.1.call-done) | data formatting | bytes 8388608 | tf_op jit(solution)/shard_map/all_gather | solution.py:68
  255.4 4.8 %gather_fusion.1 = f32[1536,128]{1,0:T(8,128)S(1)} fusion(f32[8192,128]{1,0:T(8,128)} %bitcast.117, s32[2048]{0:T(1024)S(1)} %pad_clamp_fusion), kind=kCustom, calls=%fused_computation.1.clone | custom fusion | bytes 1579008 | tf_op jit(solution)/shard_map/jit(_take)/gather | solution.py:83
  260.2 4.7 %fusion.2 = f32[16,32,128]{2,1,0:T(8,128)S(1)} fusion(f32[16,1,32,1536]{3,2,1,0:T(8,128)} %all-to-all-done, f32[1536,128]{1,0:T(8,128)S(1)} %gather_fusion.1, f32[1536]{0:T(1024)S(1)} %fusion.47, pred[1536]{0:T(1024)(128)(4,1)S(1)} %and_reduce_fusion), kind=kOutput, calls=%fused_computation.12 | convolution fusion | flops 1208352768 | bytes 4201984 | tf_op jit(solution)/shard_map/jktm,kmr->kjtr/dot_general | solution.py:84
  265.7 5.6 %reduce-scatter.6.cloned.1.call-done = f32[512,128]{0,1:T(8,128)} async-done(((f32[2048,128]{0,1:T(8,128)}), f32[512,128]{0,1:T(8,128)}) %reduce-scatter.6.cloned.1.call-update) | async-done | bytes 262160 | tf_op jit(solution)/shard_map/reduce_scatter | solution.py:70
  272.4 1.5 collective-permute-start.14
  273.9 9.0 %collective-permute-done.14 = f32[1,512,128]{1,2,0:T(8,128)S(1)} collective-permute-done((f32[1,512,128]{1,2,0:T(8,128)S(1)}, f32[1,512,128]{1,2,0:T(8,128)S(1)}, u32[]{:S(2)}, u32[]{:S(2)}) %collective-permute-start.14) | collective-permute-done | bytes 262176 | tf_op jit(solution)/shard_map/ppermute | solution.py:62
  282.9 9.6 %collective-permute-done.15 = f32[1,512,128]{1,2,0:T(8,128)S(1)} collective-permute-done((f32[1,512,128]{1,2,0:T(8,128)S(1)}, f32[1,512,128]{1,2,0:T(8,128)S(1)}, u32[]{:S(2)}, u32[]{:S(2)}) %collective-permute-start.15) | collective-permute-done | bytes 262176 | tf_op jit(solution)/shard_map/ppermute | solution.py:62
  292.5 9.1 %collective-permute-done.16 = f32[1,512,128]{1,2,0:T(8,128)S(1)} collective-permute-done((f32[1,512,128]{1,2,0:T(8,128)S(1)}, f32[1,512,128]{1,2,0:T(8,128)S(1)}, u32[]{:S(2)}, u32[]{:S(2)}) %collective-permute-start.16) | collective-permute-done | bytes 262176 | tf_op jit(solution)/shard_map/ppermute | solution.py:62
  301.6 9.1 %collective-permute-done.17 = f32[1,512,128]{1,2,0:T(8,128)S(1)} collective-permute-done((f32[1,512,128]{1,2,0:T(8,128)S(1)}, f32[1,512,128]{1,2,0:T(8,128)S(1)}, u32[]{:S(2)}, u32[]{:S(2)}) %collective-permute-start.17) | collective-permute-done | bytes 262176 | tf_op jit(solution)/shard_map/ppermute | solution.py:62
  310.7 9.4 %collective-permute-done.18 = f32[1,512,128]{1,2,0:T(8,128)S(1)} collective-permute-done((f32[1,512,128]{1,2,0:T(8,128)S(1)}, f32[1,512,128]{1,2,0:T(8,128)S(1)}, u32[]{:S(2)}, u32[]{:S(2)}) %collective-permute-start.18) | collective-permute-done | bytes 262176 | tf_op jit(solution)/shard_map/ppermute | solution.py:62
  320.0 10.5 %collective-permute-done.19 = f32[1,512,128]{1,2,0:T(8,128)S(1)} collective-permute-done((f32[1,512,128]{1,2,0:T(8,128)S(1)}, f32[1,512,128]{1,2,0:T(8,128)S(1)}, u32[]{:S(2)}, u32[]{:S(2)}) %collective-permute-start.19) | collective-permute-done | bytes 262176 | tf_op jit(solution)/shard_map/ppermute | solution.py:62
  330.5 9.1 %collective-permute-done.20 = f32[1,512,128]{1,2,0:T(8,128)S(1)} collective-permute-done((f32[1,512,128]{1,2,0:T(8,128)S(1)}, f32[1,512,128]{1,2,0:T(8,128)S(1)}, u32[]{:S(2)}, u32[]{:S(2)}) %collective-permute-start.20) | collective-permute-done | bytes 262176 | tf_op jit(solution)/shard_map/ppermute | solution.py:62
  339.8 1.9 fusion.7
  341.8 1.5 copy-done.4
  343.3 23.7 %convolution_bitcast_fusion.1 = f32[2048,128]{0,1:T(8,128)} fusion(f32[8,512,128]{1,2,0:T(8,128)S(1)} %copy-done.4, f32[8,512,2048]{2,1,0:T(8,128)} %param.10), kind=kOutput, calls=%fused_computation.18 | convolution fusion | flops 12884901888 | bytes 36700160 | tf_op jit(solution)/shard_map/dot_general | solution.py:71
  367.0 5.7 %copy.43 = f32[8,1024,128]{2,1,0:T(8,128)} copy(f32[8,1024,128]{1,2,0:T(8,128)} %all-gather.11.cloned.1.call-done) | data formatting | bytes 8388608 | tf_op jit(solution)/shard_map/all_gather | solution.py:68
  372.7 4.8 %gather_fusion.2 = f32[1536,128]{1,0:T(8,128)S(1)} fusion(f32[8192,128]{1,0:T(8,128)} %bitcast.115, s32[2048]{0:T(1024)S(1)} %pad_clamp_fusion), kind=kCustom, calls=%fused_computation.2.clone | custom fusion | bytes 1579008 | tf_op jit(solution)/shard_map/jit(_take)/gather | solution.py:83
  377.5 4.9 %fusion = f32[16,32,128]{2,1,0:T(8,128)S(1)} fusion(f32[16,1,32,1536]{3,2,1,0:T(8,128)} %all-to-all-done, f32[1536,128]{1,0:T(8,128)S(1)} %gather_fusion.2, f32[1536]{0:T(1024)S(1)} %fusion.47, pred[1536]{0:T(1024)(128)(4,1)S(1)} %and_reduce_fusion), kind=kOutput, calls=%fused_computation.10 | convolution fusion | flops 1208352768 | bytes 4201984 | tf_op jit(solution)/shard_map/jktm,kmr->kjtr/dot_general | solution.py:84
  383.2 4.5 %reduce-scatter.8.cloned.1.call-done = f32[512,128]{0,1:T(8,128)} async-done(((f32[2048,128]{0,1:T(8,128)}), f32[512,128]{0,1:T(8,128)}) %reduce-scatter.8.cloned.1.call-update) | async-done | bytes 262160 | tf_op jit(solution)/shard_map/reduce_scatter | solution.py:70
  (100 shorter events, 11.1 us)
Async XLA Ops:
  8.0 61.6 %copy-start = (f32[1,96,1536]{2,1,0:T(8,128)S(1)}, f32[1,96,1536]{2,1,0:T(8,128)}, u32[]{:S(2)}) copy-start(f32[1,96,1536]{2,1,0:T(8,128)} %param.11) | copy-start | bytes 1769476
  9.9 12.4 %collective-permute-start = (f32[1,512,128]{1,2,0:T(8,128)S(1)}, f32[1,512,128]{1,2,0:T(8,128)S(1)}, u32[]{:S(2)}, u32[]{:S(2)}) collective-permute-start(f32[1,512,128]{1,2,0:T(8,128)S(1)} %broadcast_multiply_fusion), channel_id=1, source_target_pairs={{0,4},{4,8},{8,12},{12,16},{16,20},{20,24},{24,28},{28,0},{1,5},{5... | collective-permute-start | bytes 786440 | tf_op jit(solution)/shard_map/ppermute | solution.py:62
  22.3 10.2 %collective-permute-start.1 = (f32[1,512,128]{1,2,0:T(8,128)S(1)}, f32[1,512,128]{1,2,0:T(8,128)S(1)}, u32[]{:S(2)}, u32[]{:S(2)}) collective-permute-start(f32[1,512,128]{1,2,0:T(8,128)S(1)} %collective-permute-done), channel_id=1, source_target_pairs={{0,4},{4,8},{8,12},{12,16},{16,20},{20,24},{24,28},{28,0},{1,5},{5... | collective-permute-start | bytes 786440 | tf_op jit(solution)/shard_map/ppermute | solution.py:62
  32.4 9.3 %collective-permute-start.2 = (f32[1,512,128]{1,2,0:T(8,128)S(1)}, f32[1,512,128]{1,2,0:T(8,128)S(1)}, u32[]{:S(2)}, u32[]{:S(2)}) collective-permute-start(f32[1,512,128]{1,2,0:T(8,128)S(1)} %collective-permute-done.1), channel_id=1, source_target_pairs={{0,4},{4,8},{8,12},{12,16},{16,20},{20,24},{24,28},{28,0},{1,5},{5... | collective-permute-start | bytes 786440 | tf_op jit(solution)/shard_map/ppermute | solution.py:62
  41.7 9.1 %collective-permute-start.3 = (f32[1,512,128]{1,2,0:T(8,128)S(1)}, f32[1,512,128]{1,2,0:T(8,128)S(1)}, u32[]{:S(2)}, u32[]{:S(2)}) collective-permute-start(f32[1,512,128]{1,2,0:T(8,128)S(1)} %collective-permute-done.2), channel_id=1, source_target_pairs={{0,4},{4,8},{8,12},{12,16},{16,20},{20,24},{24,28},{28,0},{1,5},{5... | collective-permute-start | bytes 786440 | tf_op jit(solution)/shard_map/ppermute | solution.py:62
  50.8 9.1 %collective-permute-start.4 = (f32[1,512,128]{1,2,0:T(8,128)S(1)}, f32[1,512,128]{1,2,0:T(8,128)S(1)}, u32[]{:S(2)}, u32[]{:S(2)}) collective-permute-start(f32[1,512,128]{1,2,0:T(8,128)S(1)} %collective-permute-done.3), channel_id=1, source_target_pairs={{0,4},{4,8},{8,12},{12,16},{16,20},{20,24},{24,28},{28,0},{1,5},{5... | collective-permute-start | bytes 786440 | tf_op jit(solution)/shard_map/ppermute | solution.py:62
  59.9 9.7 %collective-permute-start.5 = (f32[1,512,128]{1,2,0:T(8,128)S(1)}, f32[1,512,128]{1,2,0:T(8,128)S(1)}, u32[]{:S(2)}, u32[]{:S(2)}) collective-permute-start(f32[1,512,128]{1,2,0:T(8,128)S(1)} %collective-permute-done.4), channel_id=1, source_target_pairs={{0,4},{4,8},{8,12},{12,16},{16,20},{20,24},{24,28},{28,0},{1,5},{5... | collective-permute-start | bytes 786440 | tf_op jit(solution)/shard_map/ppermute | solution.py:62
  69.6 9.3 %collective-permute-start.6 = (f32[1,512,128]{1,2,0:T(8,128)S(1)}, f32[1,512,128]{1,2,0:T(8,128)S(1)}, u32[]{:S(2)}, u32[]{:S(2)}) collective-permute-start(f32[1,512,128]{1,2,0:T(8,128)S(1)} %collective-permute-done.5), channel_id=1, source_target_pairs={{0,4},{4,8},{8,12},{12,16},{16,20},{20,24},{24,28},{28,0},{1,5},{5... | collective-permute-start | bytes 786440 | tf_op jit(solution)/shard_map/ppermute | solution.py:62
  72.7 65.4 %all-to-all-start = ((f32[16,1,32,1536]{3,2,1,0:T(8,128)}), f32[16,1,32,1536]{3,2,1,0:T(8,128)}, u32[]{:S(2)}, u32[]{:S(2)}) async-start(f32[16,1,32,1536]{3,2,1,0:T(8,128)} %convolution_bitcast_fusion), calls=%async_computation.1 | async-start | bytes 6291456 | tf_op jit(solution)/shard_map/all_to_all | solution.py:45
  78.8 29.3 %all-gather.7.cloned.1.call-start = ((), (), s32[]{:S(2)}) async-start(), calls=%async_computation.7 | async-start | bytes 6291456 | tf_op jit(solution)/shard_map/all_gather | solution.py:68
  81.0 1.6 copy-start.2
  81.1 24.3 %copy-start.9 = (s32[1,1536]{1,0:T(1,128)S(1)}, s32[1,1536]{1,0:T(1,128)}, u32[]{:S(2)}) copy-start(s32[1,1536]{1,0:T(1,128)} %param.12) | copy-start | bytes 18436
  81.1 62.5 %reduce-scatter.4.cloned.1.call-start = ((), (), s32[]{:S(2)}) async-start(), calls=%async_computation.4 | async-start | bytes 1310720 | tf_op jit(solution)/shard_map/reduce_scatter | solution.py:70
  105.2 144.7 %all-gather.9.cloned.1.call-start = ((), (), s32[]{:S(2)}) async-start(), calls=%async_computation.8 | async-start | bytes 6291456 | tf_op jit(solution)/shard_map/all_gather | solution.py:68
  108.1 34.6 %copy-start.5 = (f32[16,32,512]{2,1,0:T(8,128)}, f32[16,32,512]{2,1,0:T(8,128)S(1)}, u32[]{:S(2)}) copy-start(f32[16,32,512]{2,1,0:T(8,128)S(1)} %fusion.6) | copy-start | bytes 3145732
  144.6 21.0 %collective-permute-start.7 = (f32[1,512,128]{1,2,0:T(8,128)S(1)}, f32[1,512,128]{1,2,0:T(8,128)S(1)}, u32[]{:S(2)}, u32[]{:S(2)}) collective-permute-start(f32[1,512,128]{1,2,0:T(8,128)S(1)} %fusion.43), channel_id=1, source_target_pairs={{0,4},{4,8},{8,12},{12,16},{16,20},{20,24},{24,28},{28,0},{1,5},{5... | collective-permute-start | bytes 786440 | tf_op jit(solution)/shard_map/ppermute | solution.py:62
  165.6 10.7 %collective-permute-start.8 = (f32[1,512,128]{1,2,0:T(8,128)S(1)}, f32[1,512,128]{1,2,0:T(8,128)S(1)}, u32[]{:S(2)}, u32[]{:S(2)}) collective-permute-start(f32[1,512,128]{1,2,0:T(8,128)S(1)} %collective-permute-done.7), channel_id=1, source_target_pairs={{0,4},{4,8},{8,12},{12,16},{16,20},{20,24},{24,28},{28,0},{1,5},{5... | collective-permute-start | bytes 786440 | tf_op jit(solution)/shard_map/ppermute | solution.py:62
  176.3 9.9 %collective-permute-start.9 = (f32[1,512,128]{1,2,0:T(8,128)S(1)}, f32[1,512,128]{1,2,0:T(8,128)S(1)}, u32[]{:S(2)}, u32[]{:S(2)}) collective-permute-start(f32[1,512,128]{1,2,0:T(8,128)S(1)} %collective-permute-done.8), channel_id=1, source_target_pairs={{0,4},{4,8},{8,12},{12,16},{16,20},{20,24},{24,28},{28,0},{1,5},{5... | collective-permute-start | bytes 786440 | tf_op jit(solution)/shard_map/ppermute | solution.py:62
  186.2 9.1 %collective-permute-start.10 = (f32[1,512,128]{1,2,0:T(8,128)S(1)}, f32[1,512,128]{1,2,0:T(8,128)S(1)}, u32[]{:S(2)}, u32[]{:S(2)}) collective-permute-start(f32[1,512,128]{1,2,0:T(8,128)S(1)} %collective-permute-done.9), channel_id=1, source_target_pairs={{0,4},{4,8},{8,12},{12,16},{16,20},{20,24},{24,28},{28,0},{1,5},{5... | collective-permute-start | bytes 786440 | tf_op jit(solution)/shard_map/ppermute | solution.py:62
  195.3 9.1 %collective-permute-start.11 = (f32[1,512,128]{1,2,0:T(8,128)S(1)}, f32[1,512,128]{1,2,0:T(8,128)S(1)}, u32[]{:S(2)}, u32[]{:S(2)}) collective-permute-start(f32[1,512,128]{1,2,0:T(8,128)S(1)} %collective-permute-done.10), channel_id=1, source_target_pairs={{0,4},{4,8},{8,12},{12,16},{16,20},{20,24},{24,28},{28,0},{1,5},{5... | collective-permute-start | bytes 786440 | tf_op jit(solution)/shard_map/ppermute | solution.py:62
  204.3 9.1 %collective-permute-start.12 = (f32[1,512,128]{1,2,0:T(8,128)S(1)}, f32[1,512,128]{1,2,0:T(8,128)S(1)}, u32[]{:S(2)}, u32[]{:S(2)}) collective-permute-start(f32[1,512,128]{1,2,0:T(8,128)S(1)} %collective-permute-done.11), channel_id=1, source_target_pairs={{0,4},{4,8},{8,12},{12,16},{16,20},{20,24},{24,28},{28,0},{1,5},{5... | collective-permute-start | bytes 786440 | tf_op jit(solution)/shard_map/ppermute | solution.py:62
  213.4 9.1 %collective-permute-start.13 = (f32[1,512,128]{1,2,0:T(8,128)S(1)}, f32[1,512,128]{1,2,0:T(8,128)S(1)}, u32[]{:S(2)}, u32[]{:S(2)}) collective-permute-start(f32[1,512,128]{1,2,0:T(8,128)S(1)} %collective-permute-done.12), channel_id=1, source_target_pairs={{0,4},{4,8},{8,12},{12,16},{16,20},{20,24},{24,28},{28,0},{1,5},{5... | collective-permute-start | bytes 786440 | tf_op jit(solution)/shard_map/ppermute | solution.py:62
  224.6 1.6 copy-start.3
  224.6 46.6 %reduce-scatter.6.cloned.1.call-start = ((), (), s32[]{:S(2)}) async-start(), calls=%async_computation.5 | async-start | bytes 1310720 | tf_op jit(solution)/shard_map/reduce_scatter | solution.py:70
  249.6 117.4 %all-gather.11.cloned.1.call-start = ((), (), s32[]{:S(2)}) async-start(), calls=%async_computation.9 | async-start | bytes 6291456 | tf_op jit(solution)/shard_map/all_gather | solution.py:68
  260.2 4.7 %copy-start.6 = (f32[16,32,512]{2,1,0:T(8,128)S(1)}, f32[16,32,512]{2,1,0:T(8,128)}, u32[]{:S(2)}) copy-start(f32[16,32,512]{2,1,0:T(8,128)} %copy-done.5) | copy-start | bytes 3145732
  260.2 11.1 %copy-start.8 = (f32[512,128]{0,1:T(8,128)S(1)}, f32[512,128]{0,1:T(8,128)}, u32[]{:S(2)}) copy-start(f32[512,128]{0,1:T(8,128)} %reduce-scatter.4.cloned.1.call-done) | copy-start | bytes 786436
  272.4 10.5 %collective-permute-start.14 = (f32[1,512,128]{1,2,0:T(8,128)S(1)}, f32[1,512,128]{1,2,0:T(8,128)S(1)}, u32[]{:S(2)}, u32[]{:S(2)}) collective-permute-start(f32[1,512,128]{1,2,0:T(8,128)S(1)} %bitcast.118), channel_id=1, source_target_pairs={{0,4},{4,8},{8,12},{12,16},{16,20},{20,24},{24,28},{28,0},{1,5},{5... | collective-permute-start | bytes 786440 | tf_op jit(solution)/shard_map/ppermute | solution.py:62
  282.9 9.6 %collective-permute-start.15 = (f32[1,512,128]{1,2,0:T(8,128)S(1)}, f32[1,512,128]{1,2,0:T(8,128)S(1)}, u32[]{:S(2)}, u32[]{:S(2)}) collective-permute-start(f32[1,512,128]{1,2,0:T(8,128)S(1)} %collective-permute-done.14), channel_id=1, source_target_pairs={{0,4},{4,8},{8,12},{12,16},{16,20},{20,24},{24,28},{28,0},{1,5},{5... | collective-permute-start | bytes 786440 | tf_op jit(solution)/shard_map/ppermute | solution.py:62
  292.5 9.1 %collective-permute-start.16 = (f32[1,512,128]{1,2,0:T(8,128)S(1)}, f32[1,512,128]{1,2,0:T(8,128)S(1)}, u32[]{:S(2)}, u32[]{:S(2)}) collective-permute-start(f32[1,512,128]{1,2,0:T(8,128)S(1)} %collective-permute-done.15), channel_id=1, source_target_pairs={{0,4},{4,8},{8,12},{12,16},{16,20},{20,24},{24,28},{28,0},{1,5},{5... | collective-permute-start | bytes 786440 | tf_op jit(solution)/shard_map/ppermute | solution.py:62
  301.6 9.1 %collective-permute-start.17 = (f32[1,512,128]{1,2,0:T(8,128)S(1)}, f32[1,512,128]{1,2,0:T(8,128)S(1)}, u32[]{:S(2)}, u32[]{:S(2)}) collective-permute-start(f32[1,512,128]{1,2,0:T(8,128)S(1)} %collective-permute-done.16), channel_id=1, source_target_pairs={{0,4},{4,8},{8,12},{12,16},{16,20},{20,24},{24,28},{28,0},{1,5},{5... | collective-permute-start | bytes 786440 | tf_op jit(solution)/shard_map/ppermute | solution.py:62
  310.7 9.4 %collective-permute-start.18 = (f32[1,512,128]{1,2,0:T(8,128)S(1)}, f32[1,512,128]{1,2,0:T(8,128)S(1)}, u32[]{:S(2)}, u32[]{:S(2)}) collective-permute-start(f32[1,512,128]{1,2,0:T(8,128)S(1)} %collective-permute-done.17), channel_id=1, source_target_pairs={{0,4},{4,8},{8,12},{12,16},{16,20},{20,24},{24,28},{28,0},{1,5},{5... | collective-permute-start | bytes 786440 | tf_op jit(solution)/shard_map/ppermute | solution.py:62
  320.0 10.5 %collective-permute-start.19 = (f32[1,512,128]{1,2,0:T(8,128)S(1)}, f32[1,512,128]{1,2,0:T(8,128)S(1)}, u32[]{:S(2)}, u32[]{:S(2)}) collective-permute-start(f32[1,512,128]{1,2,0:T(8,128)S(1)} %collective-permute-done.18), channel_id=1, source_target_pairs={{0,4},{4,8},{8,12},{12,16},{16,20},{20,24},{24,28},{28,0},{1,5},{5... | collective-permute-start | bytes 786440 | tf_op jit(solution)/shard_map/ppermute | solution.py:62
  330.5 9.1 %collective-permute-start.20 = (f32[1,512,128]{1,2,0:T(8,128)S(1)}, f32[1,512,128]{1,2,0:T(8,128)S(1)}, u32[]{:S(2)}, u32[]{:S(2)}) collective-permute-start(f32[1,512,128]{1,2,0:T(8,128)S(1)} %collective-permute-done.19), channel_id=1, source_target_pairs={{0,4},{4,8},{8,12},{12,16},{16,20},{20,24},{24,28},{28,0},{1,5},{5... | collective-permute-start | bytes 786440 | tf_op jit(solution)/shard_map/ppermute | solution.py:62
  341.7 1.6 copy-start.4
  341.7 45.9 %reduce-scatter.8.cloned.1.call-start = ((), (), s32[]{:S(2)}) async-start(), calls=%async_computation.6 | async-start | bytes 1310720 | tf_op jit(solution)/shard_map/reduce_scatter | solution.py:70
  377.5 4.9 %copy-start.7 = (f32[16,32,512]{2,1,0:T(8,128)S(1)}, f32[16,32,512]{2,1,0:T(8,128)}, u32[]{:S(2)}) copy-start(f32[16,32,512]{2,1,0:T(8,128)} %copy-done.5) | copy-start | bytes 3145732
  377.5 12.9 %copy-start.1 = (f32[1,96,1536]{2,1,0:T(8,128)S(1)}, f32[1,96,1536]{2,1,0:T(8,128)}, u32[]{:S(2)}) copy-start(f32[1,96,1536]{2,1,0:T(8,128)} %param.11) | copy-start | bytes 1769476
Sparse Core Ops, SparseCore 0:
  81.2 14.7 all-gather.6
  224.8 10.7 all-gather.8
  341.9 9.7 all-gather.10
Sparse Core Ops, SparseCore 1:
  105.2 25.8 reduce-scatter.3
  249.7 21.5 reduce-scatter.5
  367.1 20.5 reduce-scatter.7
